TPU v7x, 32 devices: a whole 2x2x4 slice. The times are simulated.
32 devices in a mesh: groups: 2 (over x), seq: 16 (over z, y, core).
Axes of the slice: x: 2, y: 2, z: 4, core: 2. Of those that a mesh axis runs over, the one named last changes fastest.
Arguments:
- queries: bfloat16 [4, 128, 8192], P(None, ('groups', 'seq')), parts along dimension 1, may hold values from -16 to 16
- new_keys: bfloat16 [4, 128, 1024], P(None, ('groups', 'seq')), parts along dimension 1, may hold values from -6 to 6
- new_values: bfloat16 [4, 128, 1024], P(None, ('groups', 'seq')), parts along dimension 1, may hold values from -6 to 6
- pool_keys: bfloat16 [2048, 16, 1024], P(('groups', 'seq')), parts along dimension 0, may hold values from -6 to 6
- pool_values: bfloat16 [2048, 16, 1024], P(('groups', 'seq')), parts along dimension 0, may hold values from -6 to 6
- page_table: int32 [128, 16], P(('groups', 'seq')), parts along dimension 0, may hold values from 0 to 63, as said below
- cached_len: int32 [128], P(('groups', 'seq')), parts along dimension 0, may hold values from 1 to 256
- turn_keys: bfloat16 [4, 32, 16, 1024], P(None, ('groups', 'seq')), parts along dimension 1, may hold values from -6 to 6
- turn_values: bfloat16 [4, 32, 16, 1024], P(None, ('groups', 'seq')), parts along dimension 1, may hold values from -6 to 6
- turn_lengths: int32 [32], P('groups'), parts along dimension 0, may hold values from 1 to 80, 768 in all
- turn_slot: int32 [32], P('groups'), parts along dimension 0, may hold values from 0 to 63, as said below
Outputs:
- attended: bfloat16 [4, 128, 8192], P(None, ('groups', 'seq')), parts along dimension 1
- landed_keys: bfloat16 [32, 80, 1024], P(('groups', 'seq')), parts along dimension 0
- landed_values: bfloat16 [32, 80, 1024], P(('groups', 'seq')), parts along dimension 0
There are 2 independent parts, one for each index of `groups`. A program takes and returns all parts, laid end to end along the dimension named above; each array names one. Nothing has to cross between parts.
Inputs may be any that keep to these rules, and one draw needn't show every extreme that they name: `page_table`: the 4 rows of each device's slots together hold every number of 0 to 63 exactly once. `turn_lengths`: they sum to 768; the largest is exactly 80. `turn_slot`: each block of 4 slots holds the slot of exactly one turn.
All inputs are finite; a program needn't handle non-finite values.
Results may differ from a plain program's by a relative error of at most 0.0049.
Values may be sent and summed in bfloat16 or wider, within the bound.
A program may use at most 128 MiB of HBM per device.

v0:
```python
import functools
import math

import jax
import jax.numpy as jnp
from jax import lax
from jax.experimental import pallas as pl
from jax.experimental.pallas import tpu as pltpu
from jax.sharding import PartitionSpec as P

QH = 64
KVH = 8
HD = 128
MOSTT = 80
SUB = 8
LANES = 128
NEG = -1e30
F32 = jnp.float32
BF16 = jnp.bfloat16


FACTOR = math.log2(math.e) / math.sqrt(HD)


def scores_of(qb, g, keys, biases):
    share = QH // KVH
    parts = [qb[:, pl.ds((g * share + e) * HD, HD)] for e in range(share)]
    rows = jnp.concatenate(parts, axis=0)
    raw = lax.dot_general(rows, keys, (((1,), (1,)), ((), ())), preferred_element_type=F32)
    shaped = raw.reshape(share, biases.shape[0], keys.shape[0]) * FACTOR + biases[None]
    return shaped.reshape(rows.shape[0], keys.shape[0])


def each(first, last):
    if last - first > 32:
        return pl.loop(first, last)

    def run(body):
        for k in range(first, last):
            body(k)

    return run


def finish(
    qb_hbm,
    acc_hbm,
    mx_hbm,
    sm_hbm,
    fresh_hbm,
    bias2_hbm,
    out_ref,
    lk_hbm,
    lv_hbm,
    qb,
    acc,
    mx,
    sm,
    fresh,
    bias2_ref,
    of,
    load_sem,
    sem,
):
    loads = [
        pltpu.make_async_copy(src, dst, load_sem.at[i])
        for i, (src, dst) in enumerate(
            (
                (fresh_hbm.at[0], fresh.at[0]),
                (fresh_hbm.at[1], fresh.at[1]),
                (qb_hbm, qb),
                (bias2_hbm, bias2_ref),
                (mx_hbm, mx),
                (sm_hbm, sm),
                (acc_hbm, acc),
            )
        )
    ]
    for copy in loads:
        copy.start()
    share = QH // KVH
    most_pages = lk_hbm.shape[0]
    rows_sr = qb.shape[0]
    steps, slots_here, _ = out_ref.shape
    extra = bias2_ref.shape[1]
    copies = [
        pltpu.make_async_copy(fresh.at[a, pl.ds(0, most_pages)], ref, sem.at[a])
        for a, ref in enumerate((lk_hbm, lv_hbm))
    ]
    for load, copy in zip(loads, copies):
        load.wait()
        copy.start()
    for load in loads[2:]:
        load.wait()
    bias2 = bias2_ref[...]
    for g in range(KVH):
        keys = fresh[0, :, :, pl.ds(g * HD, HD)].reshape(extra, HD)
        values = fresh[1, :, :, pl.ds(g * HD, HD)].reshape(extra, HD)
        score = scores_of(qb, g, keys, bias2)
        before = mx[:, g : g + 1]
        largest = jnp.maximum(before, jnp.max(score, axis=-1, keepdims=True))
        prob = jnp.exp2(score - largest)
        shrink = jnp.exp2(before - largest)
        total = sm[:, g : g + 1] * shrink + jnp.sum(prob, axis=-1, keepdims=True)
        mixed = acc[g] * shrink + jnp.dot(
            prob.astype(BF16), values, preferred_element_type=F32
        )
        result = mixed / total
        for e in range(share):
            of[:, pl.ds((g * share + e) * HD, HD)] = result[e * rows_sr : (e + 1) * rows_sr]
    for s in range(steps):
        out_ref[s] = of[pl.ds(s * slots_here, slots_here), :].astype(BF16)
    for copy in copies:
        copy.wait()


def kernel(
    n,
    table_ref,
    cached_ref,
    lengths_ref,
    slots_ref,
    q_hbm,
    nk_hbm,
    nv_hbm,
    pk_hbm,
    pv_hbm,
    tk_hbm,
    tv_hbm,
    qb_hbm,
    acc_hbm,
    mx_hbm,
    sm_hbm,
    fresh_hbm,
    bias2_hbm,
    qb,
    acc,
    mx,
    sm,
    fresh,
    bias2_ref,
    q_v,
    n_v,
    pk_v,
    pv_v,
    t_v,
    first_k,
    first_v,
    second,
    landing_k,
    landing_v,
    qf,
    start_s,
    pick_s,
    load_sem,
    out_sem,
    own_sem,
    send1,
    recv1,
    send2,
    recv2,
):
    me = lax.axis_index("seq")
    steps, slots_here, _ = q_hbm.shape
    group_pages, page_rows, kv_width = tk_hbm.shape
    pages_here = pk_hbm.shape[0]
    turns = lengths_ref.shape[0]
    cache_pages = table_ref.shape[1]
    lane_tiles = kv_width // LANES
    spread = (page_rows // SUB) * lane_tiles
    most_pages = -(-MOSTT // page_rows)
    fresh_span = most_pages * page_rows
    blocks = n // spread
    rows_sr = steps * slots_here
    my_block = me // spread
    first = (first_k, first_v)
    landing = (landing_k, landing_v)

    barrier = pltpu.get_barrier_semaphore()

    @each(1, n)
    def _(k):
        pl.semaphore_signal(barrier, inc=1, device_id={"seq": lax.rem(me + k, n)})

    def load(index, src, dst):
        return pltpu.make_async_copy(src, dst, load_sem.at[index])

    loads = [
        load(0, tk_hbm, t_v.at[0]),
        load(1, tv_hbm, t_v.at[1]),
        load(2, q_hbm, q_v),
        load(3, pk_hbm, pk_v),
        load(4, pv_hbm, pv_v),
        load(5, nk_hbm, n_v.at[0]),
        load(6, nv_hbm, n_v.at[1]),
    ]
    for copy in loads:
        copy.start()

    running = jnp.int32(0)
    my_length = jnp.int32(0)
    my_slot = jnp.int32(0)
    for t in range(turns):
        start_s[t] = running
        length = lengths_ref[t]
        slot = slots_ref[t]
        mine = lax.div(slot, slots_here) == me
        my_length = jnp.where(mine, length, my_length)
        my_slot = jnp.where(mine, lax.rem(slot, slots_here), my_slot)
        running = running + lax.div(length + (page_rows - 1), page_rows)

    @pl.loop(0, n)
    def _(d):
        begin = jnp.int32(0)
        for t in range(turns):
            begin = jnp.where(lax.div(slots_ref[t], slots_here) == d, start_s[t], begin)
        for j in range(most_pages):
            page = jnp.minimum(begin + j, group_pages * n - 1)
            row = lax.rem(lax.rem(page, n), spread) * group_pages + lax.div(page, n)
            pick_s[d * most_pages + j] = row

    def tile(h):
        t = lax.rem(h, spread)
        top = pl.multiple_of(lax.div(t, lane_tiles) * SUB, SUB)
        left = pl.multiple_of(lax.rem(t, lane_tiles) * LANES, LANES)
        return pl.ds(top, SUB), pl.ds(left, LANES)

    def slot_of(src):
        return pl.ds(lax.rem(src, spread) * group_pages, group_pages)

    def hand1(a, k):
        h = my_block * spread + lax.rem(lax.rem(me, spread) + k, spread)
        top, left = tile(h)
        return pltpu.make_async_remote_copy(
            src_ref=t_v.at[a, :, top, left],
            dst_ref=first[a].at[slot_of(me)],
            send_sem=send1.at[a, k],
            recv_sem=recv1.at[a, k],
            device_id={"seq": h},
        )

    def own1(a):
        top, left = tile(me)
        return pltpu.make_async_copy(
            t_v.at[a, :, top, left], first[a].at[slot_of(me)], own_sem.at[a]
        )

    def hand2(a, k):
        d = lax.rem(me + k, n)
        top, left = tile(me)
        return pltpu.make_async_remote_copy(
            src_ref=second.at[a, pl.ds(d * most_pages, most_pages)],
            dst_ref=landing[a].at[pl.ds(my_block * most_pages, most_pages), top, left],
            send_sem=send2.at[a, k],
            recv_sem=recv2.at[a, k],
            device_id={"seq": d},
        )

    def own2(a):
        top, left = tile(me)
        return pltpu.make_async_copy(
            second.at[a, pl.ds(me * most_pages, most_pages)],
            landing[a].at[pl.ds(my_block * most_pages, most_pages), top, left],
            own_sem.at[2 + a],
        )

    loads[0].wait()
    loads[1].wait()
    pl.semaphore_wait(barrier, n - 1)
    for a in range(2):

        @each(1, spread)
        def _(k, a=a):
            hand1(a, k).start()

        own1(a).start()

    loads[2].wait()
    for s in range(steps):
        qf[pl.ds(s * slots_here, slots_here), :] = q_v[s].astype(F32)
    qb[...] = qf[...].astype(BF16)

    tokens = pages_here * page_rows
    col = lax.broadcasted_iota(jnp.int32, (1, tokens), 1)
    col_page = col // page_rows
    col_row = col % page_rows
    lines = []
    for r in range(slots_here):
        room = jnp.zeros((1, tokens), jnp.int32)
        for c in range(cache_pages):
            left_over = cached_ref[r] - c * page_rows
            room = jnp.where(col_page == table_ref[r, c], left_over, room)
        lines.append(jnp.where(col_row < room, 0.0, NEG).astype(F32))
    bias = jnp.concatenate(lines * (rows_sr // slots_here), axis=0)
    def resident(g):
        keys = pk_v[:, :, pl.ds(g * HD, HD)].reshape(tokens, HD)
        values = pv_v[:, :, pl.ds(g * HD, HD)].reshape(tokens, HD)
        score = scores_of(qb, g, keys, bias)
        largest = jnp.max(score, axis=-1, keepdims=True)
        prob = jnp.exp2(score - largest)
        mx[:, g : g + 1] = largest
        sm[:, g : g + 1] = jnp.sum(prob, axis=-1, keepdims=True)
        acc[g] = jnp.dot(prob.astype(BF16), values, preferred_element_type=F32)

    loads[3].wait()
    loads[4].wait()
    half = KVH // 2
    for g in range(half):
        resident(g)

    for a in range(2):

        @each(1, spread)
        def _(k, a=a):
            hand1(a, k).wait_recv()

        own1(a).wait()
        for i in range(n * most_pages):
            second[a, i] = first[a][pick_s[i]]

        @each(1, n)
        def _(k, a=a):
            hand2(a, k).start()

        own2(a).start()

    for g in range(half, KVH):
        resident(g)

    loads[5].wait()
    loads[6].wait()
    for a in range(2):
        fresh[a, most_pages] = jnp.concatenate(
            [n_v[a, s].astype(F32) for s in range(steps)], axis=0
        ).astype(BF16)
    extra = fresh_span + rows_sr
    line = lax.broadcasted_iota(jnp.int32, (rows_sr, extra), 0)
    col = lax.broadcasted_iota(jnp.int32, (rows_sr, extra), 1)
    line_slot, line_step = line % slots_here, line // slots_here
    new_at = jnp.maximum(col - fresh_span, 0)
    fine_fresh = (line_slot == my_slot) & (col < my_length)
    fine_new = (
        (col >= fresh_span)
        & (new_at % slots_here == line_slot)
        & (new_at // slots_here <= line_step)
    )
    bias2_ref[...] = jnp.where(fine_fresh | fine_new, 0.0, NEG).astype(F32)

    stores = [
        pltpu.make_async_copy(src, dst, out_sem.at[i])
        for i, (src, dst) in enumerate(
            (
                (qb, qb_hbm),
                (acc, acc_hbm),
                (mx, mx_hbm),
                (sm, sm_hbm),
                (bias2_ref, bias2_hbm),
                (fresh.at[0], fresh_hbm.at[0]),
                (fresh.at[1], fresh_hbm.at[1]),
            )
        )
    ]
    for copy in stores[:5]:
        copy.start()

    place = lax.broadcasted_iota(jnp.int32, (page_rows, kv_width), 0)
    for a in range(2):

        @each(1, n)
        def _(k, a=a):
            hand2(a, k).wait_recv()

        own2(a).wait()
        for j in range(most_pages):
            if blocks == 1:
                block = 0
            else:
                begin = jnp.int32(0)
                for t in range(turns):
                    begin = jnp.where(
                        lax.div(slots_ref[t], slots_here) == me, start_s[t], begin
                    )
                block = lax.div(lax.rem(jnp.minimum(begin + j, group_pages * n - 1), n), spread)
            page = landing[a][block * most_pages + j]
            kept = jnp.where(place + j * page_rows < my_length, page.astype(F32), 0.0)
            fresh[a, j] = kept.astype(BF16)
        stores[5 + a].start()

    for a in range(2):

        @each(1, spread)
        def _(k, a=a):
            hand1(a, k).wait_send()

        @each(1, n)
        def _(k, a=a):
            hand2(a, k).wait_send()

    for copy in stores:
        copy.wait()


def per_device(
    queries,
    new_keys,
    new_values,
    pool_keys,
    pool_values,
    page_table,
    cached_len,
    turn_keys,
    turn_values,
    turn_lengths,
    turn_slot,
):
    n = lax.axis_size("seq")
    steps, slots_here, query_width = queries.shape
    pages_here, page_rows, kv_width = pool_keys.shape
    group_pages = turn_keys.shape[0]
    most_pages = -(-MOSTT // page_rows)
    spread = (page_rows // SUB) * (kv_width // LANES)
    blocks = n // spread
    rows_sr = steps * slots_here
    rows = rows_sr * (QH // KVH)
    paged = (group_pages, page_rows, kv_width)
    smem = pl.BlockSpec(memory_space=pltpu.SMEM)
    hbm = pl.BlockSpec(memory_space=pltpu.HBM)
    vmem = pl.BlockSpec(memory_space=pltpu.VMEM)
    extra = most_pages * page_rows + rows_sr
    parts = pl.pallas_call(
        functools.partial(kernel, n),
        out_shape=(
            jax.ShapeDtypeStruct((rows_sr, query_width), BF16),
            jax.ShapeDtypeStruct((KVH, rows, HD), F32),
            jax.ShapeDtypeStruct((rows, KVH), F32),
            jax.ShapeDtypeStruct((rows, KVH), F32),
            jax.ShapeDtypeStruct((2, most_pages + 1, page_rows, kv_width), BF16),
            jax.ShapeDtypeStruct((rows_sr, extra), F32),
        ),
        in_specs=[smem] * 4 + [hbm] * 7,
        out_specs=(hbm,) * 6,
        scratch_shapes=[
            pltpu.VMEM((rows_sr, query_width), BF16),
            pltpu.VMEM((KVH, rows, HD), F32),
            pltpu.VMEM((rows, KVH), F32),
            pltpu.VMEM((rows, KVH), F32),
            pltpu.VMEM((2, most_pages + 1, page_rows, kv_width), BF16),
            pltpu.VMEM((rows_sr, extra), F32),
            pltpu.VMEM(queries.shape, BF16),
            pltpu.VMEM((2,) + new_keys.shape, BF16),
            pltpu.VMEM(pool_keys.shape, BF16),
            pltpu.VMEM(pool_values.shape, BF16),
            pltpu.VMEM((2,) + paged, BF16),
            pltpu.VMEM((spread * group_pages, SUB, LANES), BF16),
            pltpu.VMEM((spread * group_pages, SUB, LANES), BF16),
            pltpu.VMEM((2, n * most_pages, SUB, LANES), BF16),
            pltpu.VMEM((blocks * most_pages, page_rows, kv_width), BF16),
            pltpu.VMEM((blocks * most_pages, page_rows, kv_width), BF16),
            pltpu.VMEM((rows_sr, query_width), F32),
            pltpu.SMEM(turn_lengths.shape, jnp.int32),
            pltpu.SMEM((n * most_pages,), jnp.int32),
            pltpu.SemaphoreType.DMA((7,)),
            pltpu.SemaphoreType.DMA((7,)),
            pltpu.SemaphoreType.DMA((4,)),
            pltpu.SemaphoreType.DMA((2, spread)),
            pltpu.SemaphoreType.DMA((2, spread)),
            pltpu.SemaphoreType.DMA((2, n)),
            pltpu.SemaphoreType.DMA((2, n)),
        ],
        compiler_params=pltpu.CompilerParams(
            collective_id=0, has_side_effects=True, vmem_limit_bytes=60 * 1024 * 1024
        ),
    )(
        page_table,
        cached_len,
        turn_lengths,
        turn_slot,
        queries,
        new_keys,
        new_values,
        pool_keys,
        pool_values,
        turn_keys.reshape(paged),
        turn_values.reshape(paged),
    )
    landed = jax.ShapeDtypeStruct((most_pages, page_rows, kv_width), BF16)
    attended, landed_keys, landed_values = pl.pallas_call(
        finish,
        out_shape=(jax.ShapeDtypeStruct(queries.shape, BF16), landed, landed),
        in_specs=[hbm] * 6,
        out_specs=(vmem, hbm, hbm),
        scratch_shapes=[
            pltpu.VMEM((rows_sr, query_width), BF16),
            pltpu.VMEM((KVH, rows, HD), F32),
            pltpu.VMEM((rows, KVH), F32),
            pltpu.VMEM((rows, KVH), F32),
            pltpu.VMEM((2, most_pages + 1, page_rows, kv_width), BF16),
            pltpu.VMEM((rows_sr, extra), F32),
            pltpu.VMEM((rows_sr, query_width), F32),
            pltpu.SemaphoreType.DMA((7,)),
            pltpu.SemaphoreType.DMA((2,)),
        ],
        compiler_params=pltpu.CompilerParams(vmem_limit_bytes=60 * 1024 * 1024),
    )(*parts)
    span = most_pages * page_rows
    return (
        attended,
        landed_keys.reshape(1, span, kv_width),
        landed_values.reshape(1, span, kv_width),
    )


def solution(mesh):
    in_specs = (
        P(None, ("groups", "seq"), None),
        P(None, ("groups", "seq"), None),
        P(None, ("groups", "seq"), None),
        P(("groups", "seq"), None, None),
        P(("groups", "seq"), None, None),
        P(("groups", "seq"), None),
        P(("groups", "seq")),
        P(None, ("groups", "seq"), None, None),
        P(None, ("groups", "seq"), None, None),
        P("groups"),
        P("groups"),
    )
    out_specs = (
        P(None, ("groups", "seq"), None),
        P(("groups", "seq"), None, None),
        P(("groups", "seq"), None, None),
    )
    return jax.shard_map(
        per_device, mesh=mesh, in_specs=in_specs, out_specs=out_specs, check_vma=False
    )
```

profile of v0, /device:TPU:0, one launch (start us, length us, event | category | flops | bytes accessed | tf_op | source)
XLA Modules:
  0.0 27.1 jit_solution(6681989387504422293)
XLA Ops:
  0.6 21.7 %shard_map.130 = (bf16[16,8192]{1,0:T(8,128)(2,1)}, f32[8,128,128]{2,1,0:T(8,128)}, f32[128,8]{1,0:T(8,128)}, f32[128,8]{1,0:T(8,128)}, bf16[2,6,16,1024]{3,2,1,0:T(8,128)(2,1)}, /*index=5*/f32[16,96]{1,0:T(8,128)}) custom-call(s32[4,16]{1,0:T(4,128)} %table_ref.1, s32[4]{0:T(128)} %cached_ref.1, s32[16]{0:T(128)} %lengths_ref.1, s32[16]{0:T(128)} %slots_ref.1, ...), custom_call_target="tpu_custom_call" | custom-call | tf_op jit(solution)/shard_map/pallas_call | solution.py:430
  22.3 4.7 %shard_map.131 = (bf16[4,4,8192]{2,1,0:T(4,128)(2,1)}, bf16[5,16,1024]{2,1,0:T(8,128)(2,1)}, bf16[5,16,1024]{2,1,0:T(8,128)(2,1)}) custom-call(bf16[16,8192]{1,0:T(8,128)(2,1)} %get-tuple-element.12.qb_hbm, f32[8,128,128]{2,1,0:T(8,128)} %get-tuple-element.13.acc_hbm, f32[128,8]{1,0:T(8,128)} %get-tuple-element.14.mx_hbm, ...), custom_call_target="tpu_custom_call" | custom-call | tf_op jit(solution)/shard_map/pallas_call | solution.py:487
where the time goes:
time: 27.3 us; the launch traced here: 27.1 us
  Pallas kernels  26.4 us (97%)
  between operations  0.64 us (2%)
    pallas_call x1, Pallas kernels, per_device(): pl.pallas_call(functools.partial(kernel, n), out_shape=(jax.ShapeDtypeStr...  21.7 us
    pallas_call x1, Pallas kernels, per_device(): pl.pallas_call(finish, out_shape=(jax.ShapeDtypeStruct(queries.shape, BF1...  4.74 us

commit v1 on v0

v1 whole, which is shorter than its diff:
```python
import functools
import math

import jax
import jax.numpy as jnp
from jax import lax
from jax.experimental import pallas as pl
from jax.experimental.pallas import tpu as pltpu
from jax.sharding import PartitionSpec as P

QH = 64
KVH = 8
HD = 128
MOSTT = 80
NEG = -1e30
F32 = jnp.float32
BF16 = jnp.bfloat16

FACTOR = math.log2(math.e) / math.sqrt(HD)


def scores_of(qb, g, keys, biases):
    share = QH // KVH
    parts = [qb[:, pl.ds((g * share + e) * HD, HD)] for e in range(share)]
    rows = jnp.concatenate(parts, axis=0)
    raw = lax.dot_general(rows, keys, (((1,), (1,)), ((), ())), preferred_element_type=F32)
    shaped = raw.reshape(share, biases.shape[0], keys.shape[0]) * FACTOR + biases[None]
    return shaped.reshape(rows.shape[0], keys.shape[0])


def each(first, last):
    if last - first > 32:
        return pl.loop(first, last)

    def run(body):
        for k in range(first, last):
            body(k)

    return run


def kernel(
    n,
    table_hbm,
    cached_hbm,
    lengths_hbm,
    slots_hbm,
    q_hbm,
    nk_hbm,
    nv_hbm,
    pk_hbm,
    pv_hbm,
    tk_hbm,
    tv_hbm,
    out_ref,
    lk_ref,
    lv_ref,
    qb,
    acc,
    mx,
    sm,
    pf,
    bias2_ref,
    q_v,
    n_v,
    pk_v,
    pv_v,
    t_v,
    first_k,
    first_v,
    second,
    landing,
    qf,
    table_ref,
    cached_ref,
    lengths_ref,
    slots_ref,
    start_s,
    pick_s,
    load_sem,
    send1,
    recv1,
    send2,
    recv2,
):
    me = lax.axis_index("seq")
    steps, slots_here, _ = q_hbm.shape
    group_pages, page_rows, kv_width = tk_hbm.shape
    pages_here = pk_hbm.shape[0]
    turns = lengths_ref.shape[0]
    cache_pages = table_ref.shape[1]
    spread = kv_width // HD
    most_pages = -(-MOSTT // page_rows)
    fresh_span = most_pages * page_rows
    rows_sr = steps * slots_here
    share = QH // KVH
    mine = lax.rem(me, spread)
    base = me - mine
    first = (first_k, first_v)

    barrier = pltpu.get_barrier_semaphore()

    @each(1, n)
    def _(k):
        pl.semaphore_signal(barrier, inc=1, device_id={"seq": lax.rem(me + k, n)})

    def load(index, src, dst):
        return pltpu.make_async_copy(src, dst, load_sem.at[index])

    loads = [
        load(0, tk_hbm, t_v.at[0]),
        load(1, tv_hbm, t_v.at[1]),
        load(2, q_hbm, q_v),
        load(3, pk_hbm, pk_v),
        load(4, pv_hbm, pv_v),
        load(5, nk_hbm, n_v.at[0]),
        load(6, nv_hbm, n_v.at[1]),
        load(7, lengths_hbm, lengths_ref),
        load(8, slots_hbm, slots_ref),
        load(9, table_hbm, table_ref),
        load(10, cached_hbm, cached_ref),
    ]
    for copy in loads:
        copy.start()

    def hand1(a, k):
        d = lax.rem(me + k, n)
        left = pl.multiple_of(lax.rem(d, spread) * HD, HD)
        return pltpu.make_async_remote_copy(
            src_ref=t_v.at[a, :, :, pl.ds(left, HD)],
            dst_ref=first[a].at[pl.ds(me * group_pages, group_pages)],
            send_sem=send1.at[a, k],
            recv_sem=recv1.at[a, k],
            device_id={"seq": d},
        )

    def hand2(a, k):
        to = lax.rem(mine + k, spread)
        return pltpu.make_async_remote_copy(
            src_ref=second.at[a, to],
            dst_ref=landing.at[a, mine, pl.ds(0, most_pages)],
            send_sem=send2.at[a, k],
            recv_sem=recv2.at[a, k],
            device_id={"seq": base + to},
        )

    pl.semaphore_wait(barrier, n - 1)
    left_mine = pl.multiple_of(mine * HD, HD)
    for a in range(2):
        loads[a].wait()

        @each(1, n)
        def _(k, a=a):
            hand1(a, k).start()

    for a in range(2):
        for p in range(group_pages):
            first[a][me * group_pages + p] = t_v[a, p, :, pl.ds(left_mine, HD)]

    for copy in loads[7:]:
        copy.wait()
    running = jnp.int32(0)
    my_length = jnp.int32(0)
    my_slot = jnp.int32(0)
    for t in range(turns):
        start_s[t] = running
        length = lengths_ref[t]
        slot = slots_ref[t]
        own = lax.div(slot, slots_here) == me
        my_length = jnp.where(own, length, my_length)
        my_slot = jnp.where(own, lax.rem(slot, slots_here), my_slot)
        running = running + lax.div(length + (page_rows - 1), page_rows)

    for to in range(spread):
        begin = jnp.int32(0)
        for t in range(turns):
            begin = jnp.where(lax.div(slots_ref[t], slots_here) == base + to, start_s[t], begin)
        for j in range(most_pages):
            page = jnp.minimum(begin + j, group_pages * n - 1)
            pick_s[to * most_pages + j] = lax.rem(page, n) * group_pages + lax.div(page, n)

    loads[2].wait()
    for s in range(steps):
        qf[pl.ds(s * slots_here, slots_here), :] = q_v[s].astype(F32)
    qb[...] = qf[...].astype(BF16)

    tokens = pages_here * page_rows
    col = lax.broadcasted_iota(jnp.int32, (1, tokens), 1)
    col_page = col // page_rows
    col_row = col % page_rows
    lines = []
    for r in range(slots_here):
        room = jnp.zeros((1, tokens), jnp.int32)
        for c in range(cache_pages):
            left_over = cached_ref[r] - c * page_rows
            room = jnp.where(col_page == table_ref[r, c], left_over, room)
        lines.append(jnp.where(col_row < room, 0.0, NEG).astype(F32))
    bias = jnp.concatenate(lines * (rows_sr // slots_here), axis=0)

    def resident(g):
        keys = pk_v[:, :, pl.ds(g * HD, HD)].reshape(tokens, HD)
        values = pv_v[:, :, pl.ds(g * HD, HD)].reshape(tokens, HD)
        score = scores_of(qb, g, keys, bias)
        largest = jnp.max(score, axis=-1, keepdims=True)
        prob = jnp.exp2(score - largest)
        mx[:, g : g + 1] = largest
        sm[:, g : g + 1] = jnp.sum(prob, axis=-1, keepdims=True)
        acc[g] = jnp.dot(prob.astype(BF16), values, preferred_element_type=F32)

    loads[3].wait()
    loads[4].wait()
    for g in range(KVH):
        resident(g)

    loads[5].wait()
    loads[6].wait()
    for a in range(2):
        rows = jnp.concatenate([n_v[a, s].astype(F32) for s in range(steps)], axis=0).astype(BF16)
        for g in range(KVH):
            landing[a, g, most_pages] = rows[:, g * HD : (g + 1) * HD]
    extra = fresh_span + rows_sr
    line = lax.broadcasted_iota(jnp.int32, (rows_sr, extra), 0)
    col = lax.broadcasted_iota(jnp.int32, (rows_sr, extra), 1)
    line_slot, line_step = line % slots_here, line // slots_here
    new_at = jnp.maximum(col - fresh_span, 0)
    fine_fresh = (line_slot == my_slot) & (col < my_length)
    fine_new = (
        (col >= fresh_span)
        & (new_at % slots_here == line_slot)
        & (new_at // slots_here <= line_step)
    )
    bias2_ref[...] = jnp.where(fine_fresh | fine_new, 0.0, NEG).astype(F32)

    def pass_on(a):
        @each(1, n)
        def _(k):
            hand1(a, k).wait_recv()

        for k in range(1, spread):
            to = lax.rem(mine + k, spread)
            for j in range(most_pages):
                second[a, to, j] = first[a][pick_s[to * most_pages + j]]
            hand2(a, k).start()
        for j in range(most_pages):
            landing[a, mine, j] = first[a][pick_s[mine * most_pages + j]]

    place = lax.broadcasted_iota(jnp.int32, (page_rows, HD), 0)

    def land(a, ref, g):
        for j in range(most_pages):
            page = landing[a, g, j].astype(F32)
            kept = jnp.where(place + j * page_rows < my_length, page, 0.0)
            ref[j, :, pl.ds(g * HD, HD)] = kept.astype(BF16)

    pass_on(0)
    for k in range(1, spread):
        hand2(0, k).wait_recv()
    bias2 = bias2_ref[...]
    for g in range(KVH):
        score = scores_of(qb, g, landing[0, g].reshape(extra, HD), bias2)
        before = mx[:, g : g + 1]
        largest = jnp.maximum(before, jnp.max(score, axis=-1, keepdims=True))
        prob = jnp.exp2(score - largest)
        shrink = jnp.exp2(before - largest)
        total = sm[:, g : g + 1] * shrink + jnp.sum(prob, axis=-1, keepdims=True)
        inverse = 1.0 / total
        acc[g] = acc[g] * (shrink * inverse)
        pf[g] = (prob * inverse).astype(BF16)
        land(0, lk_ref, g)

    pass_on(1)
    for k in range(1, spread):
        hand2(1, k).wait_recv()
    for g in range(KVH):
        values = landing[1, g].reshape(extra, HD)
        result = acc[g] + jnp.dot(pf[g], values, preferred_element_type=F32)
        for e in range(share):
            qf[:, pl.ds((g * share + e) * HD, HD)] = result[e * rows_sr : (e + 1) * rows_sr]
        land(1, lv_ref, g)
    for s in range(steps):
        out_ref[s] = qf[pl.ds(s * slots_here, slots_here), :].astype(BF16)

    for a in range(2):

        @each(1, n)
        def _(k, a=a):
            hand1(a, k).wait_send()

        for k in range(1, spread):
            hand2(a, k).wait_send()


def store(a_ref, b_ref, c_ref, a_hbm, b_hbm, c_hbm, sem):
    copies = [
        pltpu.make_async_copy(src, dst, sem.at[i])
        for i, (src, dst) in enumerate(((a_ref, a_hbm), (b_ref, b_hbm), (c_ref, c_hbm)))
    ]
    for copy in copies:
        copy.start()
    for copy in copies:
        copy.wait()


def per_device(
    queries,
    new_keys,
    new_values,
    pool_keys,
    pool_values,
    page_table,
    cached_len,
    turn_keys,
    turn_values,
    turn_lengths,
    turn_slot,
):
    n = lax.axis_size("seq")
    steps, slots_here, query_width = queries.shape
    pages_here, page_rows, kv_width = pool_keys.shape
    group_pages = turn_keys.shape[0]
    most_pages = -(-MOSTT // page_rows)
    spread = kv_width // HD
    rows_sr = steps * slots_here
    rows = rows_sr * (QH // KVH)
    paged = (group_pages, page_rows, kv_width)
    hbm = pl.BlockSpec(memory_space=pltpu.HBM)
    vmem = pl.BlockSpec(memory_space=pltpu.VMEM)
    extra = most_pages * page_rows + rows_sr
    landed = jax.ShapeDtypeStruct((most_pages, page_rows, kv_width), BF16)
    outs = (jax.ShapeDtypeStruct(queries.shape, BF16), landed, landed)
    held = [
        pltpu.with_memory_space_constraint(x, pltpu.HBM)
        for x in (
            page_table,
            cached_len,
            turn_lengths,
            turn_slot,
            queries,
            new_keys,
            new_values,
            pool_keys,
            pool_values,
            turn_keys.reshape(paged),
            turn_values.reshape(paged),
        )
    ]
    parts = pl.pallas_call(
        functools.partial(kernel, n),
        out_shape=outs,
        in_specs=[hbm] * 11,
        out_specs=(vmem,) * 3,
        scratch_shapes=[
            pltpu.VMEM((rows_sr, query_width), BF16),
            pltpu.VMEM((KVH, rows, HD), F32),
            pltpu.VMEM((rows, KVH), F32),
            pltpu.VMEM((rows, KVH), F32),
            pltpu.VMEM((KVH, rows, extra), BF16),
            pltpu.VMEM((rows_sr, extra), F32),
            pltpu.VMEM(queries.shape, BF16),
            pltpu.VMEM((2,) + new_keys.shape, BF16),
            pltpu.VMEM(pool_keys.shape, BF16),
            pltpu.VMEM(pool_values.shape, BF16),
            pltpu.VMEM((2,) + paged, BF16),
            pltpu.VMEM((n * group_pages, page_rows, HD), BF16),
            pltpu.VMEM((n * group_pages, page_rows, HD), BF16),
            pltpu.VMEM((2, spread, most_pages, page_rows, HD), BF16),
            pltpu.VMEM((2, spread, most_pages + 1, page_rows, HD), BF16),
            pltpu.VMEM((rows_sr, query_width), F32),
            pltpu.SMEM(page_table.shape, jnp.int32),
            pltpu.SMEM(cached_len.shape, jnp.int32),
            pltpu.SMEM(turn_lengths.shape, jnp.int32),
            pltpu.SMEM(turn_slot.shape, jnp.int32),
            pltpu.SMEM(turn_lengths.shape, jnp.int32),
            pltpu.SMEM((spread * most_pages,), jnp.int32),
            pltpu.SemaphoreType.DMA((11,)),
            pltpu.SemaphoreType.DMA((2, n)),
            pltpu.SemaphoreType.DMA((2, n)),
            pltpu.SemaphoreType.DMA((2, spread)),
            pltpu.SemaphoreType.DMA((2, spread)),
        ],
        compiler_params=pltpu.CompilerParams(
            collective_id=0, has_side_effects=True, vmem_limit_bytes=24 * 1024 * 1024
        ),
    )(*held)
    attended, landed_keys, landed_values = pl.pallas_call(
        store,
        out_shape=outs,
        in_specs=[vmem] * 3,
        out_specs=(hbm,) * 3,
        scratch_shapes=[pltpu.SemaphoreType.DMA((3,))],
        compiler_params=pltpu.CompilerParams(vmem_limit_bytes=8 * 1024 * 1024),
    )(*parts)
    span = most_pages * page_rows
    return (
        attended,
        landed_keys.reshape(1, span, kv_width),
        landed_values.reshape(1, span, kv_width),
    )


def solution(mesh):
    in_specs = (
        P(None, ("groups", "seq"), None),
        P(None, ("groups", "seq"), None),
        P(None, ("groups", "seq"), None),
        P(("groups", "seq"), None, None),
        P(("groups", "seq"), None, None),
        P(("groups", "seq"), None),
        P(("groups", "seq")),
        P(None, ("groups", "seq"), None, None),
        P(None, ("groups", "seq"), None, None),
        P("groups"),
        P("groups"),
    )
    out_specs = (
        P(None, ("groups", "seq"), None),
        P(("groups", "seq"), None, None),
        P(("groups", "seq"), None, None),
    )
    return jax.shard_map(
        per_device, mesh=mesh, in_specs=in_specs, out_specs=out_specs, check_vma=False
    )
```

time: 27.3 us -> 28 us (1.026)
  Pallas kernels: 26.4 us -> 27.2 us
    pallas_call x2, Pallas kernels: 26.4 us -> 27.2 us  [the longest x1 26.4 us: per_device(): pl.pallas_call(functools.partial(kernel, n), out_shape=outs, in_specs=[hb...]
where the time goes in v1:
time: 28 us; the launch traced here: 27.9 us
  Pallas kernels  27.2 us (97%)
  between operations  0.64 us (2%)
    pallas_call x1, Pallas kernels, per_device(): pl.pallas_call(functools.partial(kernel, n), out_shape=outs, in_specs=[hb...  26.4 us
    pallas_call x1, Pallas kernels, per_device(): pl.pallas_call(store, out_shape=outs, in_specs=[vmem] * 3, out_specs=(hbm...  0.84 us

profile of v1, /device:TPU:0, one launch (start us, length us, event | category | flops | bytes accessed | tf_op | source)
XLA Modules:
  0.0 27.9 jit_solution(5843339468749855779)
XLA Ops:
  0.6 26.4 %shard_map.130 = (bf16[4,4,8192]{2,1,0:T(4,128)(2,1)S(1)}, bf16[5,16,1024]{2,1,0:T(8,128)(2,1)S(1)}, bf16[5,16,1024]{2,1,0:T(8,128)(2,1)S(1)}) custom-call(s32[4,16]{1,0:T(4,128)} %table_hbm.1, s32[4]{0:T(128)} %cached_hbm.1, s32[16]{0:T(128)} %lengths_hbm.1, s32[16]{0:T(128)} %slots_hbm.1, bf16[4,4,8192]{2,1,0:T(4,128)(2,1)} %q_hbm.1, ...), custom_call_target="tpu_custom_call" | custom-call | tf_op jit(solution)/shard_map/pallas_call | solution.py:347
  27.0 0.8 %shard_map.131 = (bf16[4,4,8192]{2,1,0:T(4,128)(2,1)}, bf16[5,16,1024]{2,1,0:T(8,128)(2,1)}, bf16[5,16,1024]{2,1,0:T(8,128)(2,1)}) custom-call(bf16[4,4,8192]{2,1,0:T(4,128)(2,1)S(1)} %get-tuple-element.9.a_ref, bf16[5,16,1024]{2,1,0:T(8,128)(2,1)S(1)} %get-tuple-element.10.b_ref, bf16[5,16,1024]{2,1,0:T(8,128)(2,1)S(1)} %get-tuple-element.11.c_ref), custom_call_target="tpu_custom_call" | custom-call | tf_op jit(solution)/shard_map/pallas_call | solution.py:385

commit v2 on v1

--- a/solution.py
+++ b/solution.py
@@ -12,6 +12,7 @@
 KVH = 8
 HD = 128
 MOSTT = 80
+SUB = 8
 NEG = -1e30
 F32 = jnp.float32
 BF16 = jnp.bfloat16
@@ -70,6 +71,7 @@
     first_v,
     second,
     landing,
+    fresh,
     qf,
     table_ref,
     cached_ref,
@@ -78,6 +80,7 @@
     start_s,
     pick_s,
     load_sem,
+    own_sem,
     send1,
     recv1,
     send2,
@@ -89,14 +92,17 @@
     pages_here = pk_hbm.shape[0]
     turns = lengths_ref.shape[0]
     cache_pages = table_ref.shape[1]
-    spread = kv_width // HD
+    lane_tiles = kv_width // HD
+    spread = (page_rows // SUB) * lane_tiles
     most_pages = -(-MOSTT // page_rows)
     fresh_span = most_pages * page_rows
+    blocks = n // spread
     rows_sr = steps * slots_here
     share = QH // KVH
-    mine = lax.rem(me, spread)
-    base = me - mine
+    my_block = me // spread
     first = (first_k, first_v)
+    if blocks == 1:
+        fresh = landing.at[:, 0]
 
     barrier = pltpu.get_barrier_semaphore()
 
@@ -123,39 +129,59 @@
     for copy in loads:
         copy.start()
 
+    def tile(h):
+        t = lax.rem(h, spread)
+        top = pl.multiple_of(lax.div(t, lane_tiles) * SUB, SUB)
+        return pl.ds(top, SUB), lax.rem(t, lane_tiles)
+
+    def tile_of(a, h):
+        top, head = tile(h)
+        return t_v.at[a, :, top, pl.ds(pl.multiple_of(head * HD, HD), HD)]
+
+    def slot_of(src):
+        return pl.ds(lax.rem(src, spread) * group_pages, group_pages)
+
     def hand1(a, k):
-        d = lax.rem(me + k, n)
-        left = pl.multiple_of(lax.rem(d, spread) * HD, HD)
+        h = my_block * spread + lax.rem(lax.rem(me, spread) + k, spread)
         return pltpu.make_async_remote_copy(
-            src_ref=t_v.at[a, :, :, pl.ds(left, HD)],
-            dst_ref=first[a].at[pl.ds(me * group_pages, group_pages)],
+            src_ref=tile_of(a, h),
+            dst_ref=first[a].at[slot_of(me)],
             send_sem=send1.at[a, k],
             recv_sem=recv1.at[a, k],
+            device_id={"seq": h},
+        )
+
+    def own1(a):
+        return pltpu.make_async_copy(tile_of(a, me), first[a].at[slot_of(me)], own_sem.at[a])
+
+    def place_at(a):
+        top, head = tile(me)
+        return landing.at[a, my_block, head, pl.ds(0, most_pages), top]
+
+    def hand2(a, k):
+        d = lax.rem(me + k, n)
+        return pltpu.make_async_remote_copy(
+            src_ref=second.at[a, pl.ds(d * most_pages, most_pages)],
+            dst_ref=place_at(a),
+            send_sem=send2.at[a, k],
+            recv_sem=recv2.at[a, k],
             device_id={"seq": d},
         )
 
-    def hand2(a, k):
-        to = lax.rem(mine + k, spread)
-        return pltpu.make_async_remote_copy(
-            src_ref=second.at[a, to],
-            dst_ref=landing.at[a, mine, pl.ds(0, most_pages)],
-            send_sem=send2.at[a, k],
-            recv_sem=recv2.at[a, k],
-            device_id={"seq": base + to},
+    def own2(a):
+        return pltpu.make_async_copy(
+            second.at[a, pl.ds(me * most_pages, most_pages)], place_at(a), own_sem.at[2 + a]
         )
 
     pl.semaphore_wait(barrier, n - 1)
-    left_mine = pl.multiple_of(mine * HD, HD)
     for a in range(2):
         loads[a].wait()
 
-        @each(1, n)
+        @each(1, spread)
         def _(k, a=a):
             hand1(a, k).start()
 
-    for a in range(2):
-        for p in range(group_pages):
-            first[a][me * group_pages + p] = t_v[a, p, :, pl.ds(left_mine, HD)]
+        own1(a).start()
 
     for copy in loads[7:]:
         copy.wait()
@@ -171,13 +197,15 @@
         my_slot = jnp.where(own, lax.rem(slot, slots_here), my_slot)
         running = running + lax.div(length + (page_rows - 1), page_rows)
 
-    for to in range(spread):
+    @pl.loop(0, n)
+    def _(d):
         begin = jnp.int32(0)
         for t in range(turns):
-            begin = jnp.where(lax.div(slots_ref[t], slots_here) == base + to, start_s[t], begin)
+            begin = jnp.where(lax.div(slots_ref[t], slots_here) == d, start_s[t], begin)
         for j in range(most_pages):
             page = jnp.minimum(begin + j, group_pages * n - 1)
-            pick_s[to * most_pages + j] = lax.rem(page, n) * group_pages + lax.div(page, n)
+            row = lax.rem(lax.rem(page, n), spread) * group_pages + lax.div(page, n)
+            pick_s[d * most_pages + j] = row
 
     loads[2].wait()
     for s in range(steps):
@@ -217,7 +245,7 @@
     for a in range(2):
         rows = jnp.concatenate([n_v[a, s].astype(F32) for s in range(steps)], axis=0).astype(BF16)
         for g in range(KVH):
-            landing[a, g, most_pages] = rows[:, g * HD : (g + 1) * HD]
+            fresh[a, g, most_pages] = rows[:, g * HD : (g + 1) * HD]
     extra = fresh_span + rows_sr
     line = lax.broadcasted_iota(jnp.int32, (rows_sr, extra), 0)
     col = lax.broadcasted_iota(jnp.int32, (rows_sr, extra), 1)
@@ -232,48 +260,64 @@
     bias2_ref[...] = jnp.where(fine_fresh | fine_new, 0.0, NEG).astype(F32)
 
     def pass_on(a):
+        @each(1, spread)
+        def _(k):
+            hand1(a, k).wait_recv()
+
+        own1(a).wait()
+        for i in range(n * most_pages):
+            second[a, i] = first[a][pick_s[i]]
+
         @each(1, n)
         def _(k):
-            hand1(a, k).wait_recv()
-
-        for k in range(1, spread):
-            to = lax.rem(mine + k, spread)
+            hand2(a, k).start()
+
+        own2(a).start()
+
+    def arrive(a):
+        @each(1, n)
+        def _(k):
+            hand2(a, k).wait_recv()
+
+        own2(a).wait()
+        if blocks > 1:
+            begin = jnp.int32(0)
+            for t in range(turns):
+                begin = jnp.where(lax.div(slots_ref[t], slots_here) == me, start_s[t], begin)
             for j in range(most_pages):
-                second[a, to, j] = first[a][pick_s[to * most_pages + j]]
-            hand2(a, k).start()
-        for j in range(most_pages):
-            landing[a, mine, j] = first[a][pick_s[mine * most_pages + j]]
+                page = jnp.minimum(begin + j, group_pages * n - 1)
+                block = lax.div(lax.rem(page, n), spread)
+                for g in range(KVH):
+                    fresh[a, g, j] = landing[a, block, g, j]
 
     place = lax.broadcasted_iota(jnp.int32, (page_rows, HD), 0)
 
     def land(a, ref, g):
         for j in range(most_pages):
-            page = landing[a, g, j].astype(F32)
+            page = fresh[a, g, j].astype(F32)
             kept = jnp.where(place + j * page_rows < my_length, page, 0.0)
             ref[j, :, pl.ds(g * HD, HD)] = kept.astype(BF16)
 
     pass_on(0)
-    for k in range(1, spread):
-        hand2(0, k).wait_recv()
+    pass_on(1)
+    arrive(0)
     bias2 = bias2_ref[...]
     for g in range(KVH):
-        score = scores_of(qb, g, landing[0, g].reshape(extra, HD), bias2)
+        score = scores_of(qb, g, fresh[0, g].reshape(extra, HD), bias2)
         before = mx[:, g : g + 1]
         largest = jnp.maximum(before, jnp.max(score, axis=-1, keepdims=True))
         prob = jnp.exp2(score - largest)
         shrink = jnp.exp2(before - largest)
-        total = sm[:, g : g + 1] * shrink + jnp.sum(prob, axis=-1, keepdims=True)
-        inverse = 1.0 / total
-        acc[g] = acc[g] * (shrink * inverse)
-        pf[g] = (prob * inverse).astype(BF16)
+        sm[:, g : g + 1] = sm[:, g : g + 1] * shrink + jnp.sum(prob, axis=-1, keepdims=True)
+        acc[g] = acc[g] * shrink
+        pf[g] = prob.astype(BF16)
         land(0, lk_ref, g)
 
-    pass_on(1)
-    for k in range(1, spread):
-        hand2(1, k).wait_recv()
+    arrive(1)
     for g in range(KVH):
-        values = landing[1, g].reshape(extra, HD)
-        result = acc[g] + jnp.dot(pf[g], values, preferred_element_type=F32)
+        values = fresh[1, g].reshape(extra, HD)
+        mixed = acc[g] + jnp.dot(pf[g], values, preferred_element_type=F32)
+        result = mixed / sm[:, g : g + 1]
         for e in range(share):
             qf[:, pl.ds((g * share + e) * HD, HD)] = result[e * rows_sr : (e + 1) * rows_sr]
         land(1, lv_ref, g)
@@ -282,11 +326,12 @@
 
     for a in range(2):
 
+        @each(1, spread)
+        def _(k, a=a):
+            hand1(a, k).wait_send()
+
         @each(1, n)
         def _(k, a=a):
-            hand1(a, k).wait_send()
-
-        for k in range(1, spread):
             hand2(a, k).wait_send()
 
 
@@ -319,7 +364,8 @@
     pages_here, page_rows, kv_width = pool_keys.shape
     group_pages = turn_keys.shape[0]
     most_pages = -(-MOSTT // page_rows)
-    spread = kv_width // HD
+    spread = (page_rows // SUB) * (kv_width // HD)
+    blocks = n // spread
     rows_sr = steps * slots_here
     rows = rows_sr * (QH // KVH)
     paged = (group_pages, page_rows, kv_width)
@@ -361,22 +407,24 @@
             pltpu.VMEM(pool_keys.shape, BF16),
             pltpu.VMEM(pool_values.shape, BF16),
             pltpu.VMEM((2,) + paged, BF16),
-            pltpu.VMEM((n * group_pages, page_rows, HD), BF16),
-            pltpu.VMEM((n * group_pages, page_rows, HD), BF16),
-            pltpu.VMEM((2, spread, most_pages, page_rows, HD), BF16),
-            pltpu.VMEM((2, spread, most_pages + 1, page_rows, HD), BF16),
+            pltpu.VMEM((spread * group_pages, SUB, HD), BF16),
+            pltpu.VMEM((spread * group_pages, SUB, HD), BF16),
+            pltpu.VMEM((2, n * most_pages, SUB, HD), BF16),
+            pltpu.VMEM((2, blocks, KVH, most_pages + 1, page_rows, HD), BF16),
+            pltpu.VMEM((2, KVH, most_pages + 1, page_rows, HD) if blocks > 1 else (8, HD), BF16),
             pltpu.VMEM((rows_sr, query_width), F32),
             pltpu.SMEM(page_table.shape, jnp.int32),
             pltpu.SMEM(cached_len.shape, jnp.int32),
             pltpu.SMEM(turn_lengths.shape, jnp.int32),
             pltpu.SMEM(turn_slot.shape, jnp.int32),
             pltpu.SMEM(turn_lengths.shape, jnp.int32),
-            pltpu.SMEM((spread * most_pages,), jnp.int32),
+            pltpu.SMEM((n * most_pages,), jnp.int32),
             pltpu.SemaphoreType.DMA((11,)),
+            pltpu.SemaphoreType.DMA((4,)),
+            pltpu.SemaphoreType.DMA((2, spread)),
+            pltpu.SemaphoreType.DMA((2, spread)),
             pltpu.SemaphoreType.DMA((2, n)),
             pltpu.SemaphoreType.DMA((2, n)),
-            pltpu.SemaphoreType.DMA((2, spread)),
-            pltpu.SemaphoreType.DMA((2, spread)),
         ],
         compiler_params=pltpu.CompilerParams(
             collective_id=0, has_side_effects=True, vmem_limit_bytes=24 * 1024 * 1024

time: 28 us -> 22.4 us (0.80)
  Pallas kernels: 27.2 us -> 21.5 us
    pallas_call x1, Pallas kernels: 26.4 us -> 20.6 us  [per_device(): pl.pallas_call(functools.partial(kernel, n), out_shape=outs, in_specs=[hb...]
where the time goes in v2:
time: 22.4 us; the launch traced here: 22.1 us
  Pallas kernels  21.5 us (96%)
  between operations  0.64 us (3%)
    pallas_call x1, Pallas kernels, per_device(): pl.pallas_call(functools.partial(kernel, n), out_shape=outs, in_specs=[hb...  20.6 us
    pallas_call x1, Pallas kernels, per_device(): pl.pallas_call(store, out_shape=outs, in_specs=[vmem] * 3, out_specs=(hbm...  0.84 us

profile of v2, /device:TPU:0, one launch (start us, length us, event | category | flops | bytes accessed | tf_op | source)
XLA Modules:
  0.0 22.1 jit_solution(6067218645771604942)
XLA Ops:
  0.6 20.6 %shard_map.130 = (bf16[4,4,8192]{2,1,0:T(4,128)(2,1)S(1)}, bf16[5,16,1024]{2,1,0:T(8,128)(2,1)S(1)}, bf16[5,16,1024]{2,1,0:T(8,128)(2,1)S(1)}) custom-call(s32[4,16]{1,0:T(4,128)} %table_hbm.1, s32[4]{0:T(128)} %cached_hbm.1, s32[16]{0:T(128)} %lengths_hbm.1, s32[16]{0:T(128)} %slots_hbm.1, bf16[4,4,8192]{2,1,0:T(4,128)(2,1)} %q_hbm.1, ...), custom_call_target="tpu_custom_call" | custom-call | tf_op jit(solution)/shard_map/pallas_call | solution.py:393
  21.3 0.8 %shard_map.131 = (bf16[4,4,8192]{2,1,0:T(4,128)(2,1)}, bf16[5,16,1024]{2,1,0:T(8,128)(2,1)}, bf16[5,16,1024]{2,1,0:T(8,128)(2,1)}) custom-call(bf16[4,4,8192]{2,1,0:T(4,128)(2,1)S(1)} %get-tuple-element.9.a_ref, bf16[5,16,1024]{2,1,0:T(8,128)(2,1)S(1)} %get-tuple-element.10.b_ref, bf16[5,16,1024]{2,1,0:T(8,128)(2,1)S(1)} %get-tuple-element.11.c_ref), custom_call_target="tpu_custom_call" | custom-call | tf_op jit(solution)/shard_map/pallas_call | solution.py:433

commit v3 on v2

--- a/solution.py
+++ b/solution.py
@@ -13,6 +13,7 @@
 HD = 128
 MOSTT = 80
 SUB = 8
+PLANE = 4
 NEG = -1e30
 F32 = jnp.float32
 BF16 = jnp.bfloat16
@@ -81,6 +82,7 @@
     pick_s,
     load_sem,
     own_sem,
+    ready,
     send1,
     recv1,
     send2,
@@ -106,9 +108,9 @@
 
     barrier = pltpu.get_barrier_semaphore()
 
-    @each(1, n)
-    def _(k):
-        pl.semaphore_signal(barrier, inc=1, device_id={"seq": lax.rem(me + k, n)})
+    @pl.loop(me + 1, n)
+    def _(d):
+        pl.semaphore_signal(barrier, inc=1, device_id={"seq": d})
 
     def load(index, src, dst):
         return pltpu.make_async_copy(src, dst, load_sem.at[index])
@@ -141,13 +143,12 @@
     def slot_of(src):
         return pl.ds(lax.rem(src, spread) * group_pages, group_pages)
 
-    def hand1(a, k):
-        h = my_block * spread + lax.rem(lax.rem(me, spread) + k, spread)
+    def hand1(a, h, src):
         return pltpu.make_async_remote_copy(
             src_ref=tile_of(a, h),
             dst_ref=first[a].at[slot_of(me)],
-            send_sem=send1.at[a, k],
-            recv_sem=recv1.at[a, k],
+            send_sem=send1.at[a, lax.rem(h, spread)],
+            recv_sem=recv1.at[a, lax.rem(src, spread)],
             device_id={"seq": h},
         )
 
@@ -158,13 +159,12 @@
         top, head = tile(me)
         return landing.at[a, my_block, head, pl.ds(0, most_pages), top]
 
-    def hand2(a, k):
-        d = lax.rem(me + k, n)
+    def hand2(a, d, src):
         return pltpu.make_async_remote_copy(
             src_ref=second.at[a, pl.ds(d * most_pages, most_pages)],
             dst_ref=place_at(a),
-            send_sem=send2.at[a, k],
-            recv_sem=recv2.at[a, k],
+            send_sem=send2.at[a, d],
+            recv_sem=recv2.at[a, src],
             device_id={"seq": d},
         )
 
@@ -173,15 +173,55 @@
             second.at[a, pl.ds(me * most_pages, most_pages)], place_at(a), own_sem.at[2 + a]
         )
 
-    pl.semaphore_wait(barrier, n - 1)
-    for a in range(2):
-        loads[a].wait()
-
-        @each(1, spread)
-        def _(k, a=a):
-            hand1(a, k).start()
-
-        own1(a).start()
+    start_block = my_block * spread
+    my_plane = me // PLANE
+    in_plane = lax.rem(me, PLANE)
+
+    def partner(i):
+        return (i // PLANE) * PLANE + lax.rem(in_plane + i, PLANE)
+
+    def below(first_device, act):
+        @pl.loop(first_device, my_plane * PLANE)
+        def _(i):
+            act(partner(i))
+
+        for k in range(1, PLANE):
+            d = partner(my_plane * PLANE + k)
+            pl.when(d < me)(functools.partial(act, d))
+
+    def above(last_device, act):
+        for k in range(1, PLANE):
+            d = partner(my_plane * PLANE + k)
+            pl.when(d > me)(functools.partial(act, d))
+
+        @pl.loop((my_plane + 1) * PLANE, last_device)
+        def _(i):
+            act(partner(i))
+
+    def tell(d):
+        pl.semaphore_signal(ready.at[me], inc=1, device_id={"seq": d})
+
+    def send1_to(a):
+        def act(d):
+            hand1(a, d, me).start()
+
+        return act
+
+    def send1_ready(a):
+        def act(d):
+            pl.semaphore_wait(ready.at[d], 1)
+            hand1(a, d, me).start()
+
+        return act
+
+    @pl.when(me > 0)
+    def _():
+        pl.semaphore_wait(barrier, me)
+
+    below(0, tell)
+    loads[0].wait()
+    below(start_block, send1_to(0))
+    own1(0).start()
 
     for copy in loads[7:]:
         copy.wait()
@@ -237,6 +277,17 @@
 
     loads[3].wait()
     loads[4].wait()
+    above(start_block + spread, send1_ready(0))
+    loads[1].wait()
+    below(start_block, send1_to(1))
+    above(start_block + spread, send1_to(1))
+    own1(1).start()
+    if blocks > 1:
+
+        @pl.loop(start_block + spread, n)
+        def _(d):
+            pl.semaphore_wait(ready.at[d], 1)
+
     for g in range(KVH):
         resident(g)
 
@@ -262,22 +313,26 @@
     def pass_on(a):
         @each(1, spread)
         def _(k):
-            hand1(a, k).wait_recv()
+            src = start_block + lax.rem(lax.rem(me, spread) + k, spread)
+            hand1(a, src, src).wait_recv()
 
         own1(a).wait()
         for i in range(n * most_pages):
             second[a, i] = first[a][pick_s[i]]
 
-        @each(1, n)
-        def _(k):
-            hand2(a, k).start()
+        def act(d):
+            hand2(a, d, me).start()
+
+        for k in range(1, n):
+            act(lax.rem(me + k, n))
 
         own2(a).start()
 
     def arrive(a):
         @each(1, n)
         def _(k):
-            hand2(a, k).wait_recv()
+            src = lax.rem(me + k, n)
+            hand2(a, src, src).wait_recv()
 
         own2(a).wait()
         if blocks > 1:
@@ -328,11 +383,12 @@
 
         @each(1, spread)
         def _(k, a=a):
-            hand1(a, k).wait_send()
+            h = start_block + lax.rem(lax.rem(me, spread) + k, spread)
+            hand1(a, h, me).wait_send()
 
         @each(1, n)
         def _(k, a=a):
-            hand2(a, k).wait_send()
+            hand2(a, lax.rem(me + k, n), me).wait_send()
 
 
 def store(a_ref, b_ref, c_ref, a_hbm, b_hbm, c_hbm, sem):
@@ -421,6 +477,7 @@
             pltpu.SMEM((n * most_pages,), jnp.int32),
             pltpu.SemaphoreType.DMA((11,)),
             pltpu.SemaphoreType.DMA((4,)),
+            pltpu.SemaphoreType.REGULAR((n,)),
             pltpu.SemaphoreType.DMA((2, spread)),
             pltpu.SemaphoreType.DMA((2, spread)),
             pltpu.SemaphoreType.DMA((2, n)),

time: 22.4 us -> 22.2 us (level)
  no operation moved by 1% of the time
where the time goes in v3:
time: 22.2 us; the launch traced here: 22 us
  Pallas kernels  21.4 us (96%)
  between operations  0.64 us (3%)
    pallas_call x1, Pallas kernels, per_device(): pl.pallas_call(functools.partial(kernel, n), out_shape=outs, in_specs=[hb...  20.6 us
    pallas_call x1, Pallas kernels, per_device(): pl.pallas_call(store, out_shape=outs, in_specs=[vmem] * 3, out_specs=(hbm...  0.84 us

profile of v3, /device:TPU:0, one launch (start us, length us, event | category | flops | bytes accessed | tf_op | source)
XLA Modules:
  0.0 22.0 jit_solution(15892468053721105621)
XLA Ops:
  0.6 20.6 %shard_map.130 = (bf16[4,4,8192]{2,1,0:T(4,128)(2,1)S(1)}, bf16[5,16,1024]{2,1,0:T(8,128)(2,1)S(1)}, bf16[5,16,1024]{2,1,0:T(8,128)(2,1)S(1)}) custom-call(s32[4,16]{1,0:T(4,128)} %table_hbm.1, s32[4]{0:T(128)} %cached_hbm.1, s32[16]{0:T(128)} %lengths_hbm.1, s32[16]{0:T(128)} %slots_hbm.1, bf16[4,4,8192]{2,1,0:T(4,128)(2,1)} %q_hbm.1, ...), custom_call_target="tpu_custom_call" | custom-call | tf_op jit(solution)/shard_map/pallas_call | solution.py:449
  21.2 0.8 %shard_map.131 = (bf16[4,4,8192]{2,1,0:T(4,128)(2,1)}, bf16[5,16,1024]{2,1,0:T(8,128)(2,1)}, bf16[5,16,1024]{2,1,0:T(8,128)(2,1)}) custom-call(bf16[4,4,8192]{2,1,0:T(4,128)(2,1)S(1)} %get-tuple-element.9.a_ref, bf16[5,16,1024]{2,1,0:T(8,128)(2,1)S(1)} %get-tuple-element.10.b_ref, bf16[5,16,1024]{2,1,0:T(8,128)(2,1)S(1)} %get-tuple-element.11.c_ref), custom_call_target="tpu_custom_call" | custom-call | tf_op jit(solution)/shard_map/pallas_call | solution.py:490

commit v4 on v3

--- a/solution.py
+++ b/solution.py
@@ -368,8 +368,15 @@
         pf[g] = prob.astype(BF16)
         land(0, lk_ref, g)
 
-    arrive(1)
-    for g in range(KVH):
+    if blocks > 1:
+        arrive(1)
+    else:
+        own2(1).wait()
+    for g in (0, 1, 2, 3, 4, 5, 6, 7):
+        if blocks == 1 and g in {0: (0, 1, 2, 3), 4: (4, 5, 6, 7)}:
+            for src in range(n):
+                if src % lane_tiles in {0: (0, 1, 2, 3), 4: (4, 5, 6, 7)}[g]:
+                    pl.when(src != me)(hand2(1, src, src).wait_recv)
         values = fresh[1, g].reshape(extra, HD)
         mixed = acc[g] + jnp.dot(pf[g], values, preferred_element_type=F32)
         result = mixed / sm[:, g : g + 1]

time: 22.2 us -> 22.1 us (level)
  no operation moved by 1% of the time
where the time goes in v4:
time: 22.1 us; the launch traced here: 22 us
  Pallas kernels  21.3 us (96%)
  between operations  0.64 us (3%)
    pallas_call x1, Pallas kernels, per_device(): pl.pallas_call(functools.partial(kernel, n), out_shape=outs, in_specs=[hb...  20.5 us
    pallas_call x1, Pallas kernels, per_device(): pl.pallas_call(store, out_shape=outs, in_specs=[vmem] * 3, out_specs=(hbm...  0.84 us

profile of v4, /device:TPU:0, one launch (start us, length us, event | category | flops | bytes accessed | tf_op | source)
XLA Modules:
  0.0 22.0 jit_solution(10222626101862746362)
XLA Ops:
  0.6 20.5 %shard_map.130 = (bf16[4,4,8192]{2,1,0:T(4,128)(2,1)S(1)}, bf16[5,16,1024]{2,1,0:T(8,128)(2,1)S(1)}, bf16[5,16,1024]{2,1,0:T(8,128)(2,1)S(1)}) custom-call(s32[4,16]{1,0:T(4,128)} %table_hbm.1, s32[4]{0:T(128)} %cached_hbm.1, s32[16]{0:T(128)} %lengths_hbm.1, s32[16]{0:T(128)} %slots_hbm.1, bf16[4,4,8192]{2,1,0:T(4,128)(2,1)} %q_hbm.1, ...), custom_call_target="tpu_custom_call" | custom-call | tf_op jit(solution)/shard_map/pallas_call | solution.py:456
  21.1 0.8 %shard_map.131 = (bf16[4,4,8192]{2,1,0:T(4,128)(2,1)}, bf16[5,16,1024]{2,1,0:T(8,128)(2,1)}, bf16[5,16,1024]{2,1,0:T(8,128)(2,1)}) custom-call(bf16[4,4,8192]{2,1,0:T(4,128)(2,1)S(1)} %get-tuple-element.9.a_ref, bf16[5,16,1024]{2,1,0:T(8,128)(2,1)S(1)} %get-tuple-element.10.b_ref, bf16[5,16,1024]{2,1,0:T(8,128)(2,1)S(1)} %get-tuple-element.11.c_ref), custom_call_target="tpu_custom_call" | custom-call | tf_op jit(solution)/shard_map/pallas_call | solution.py:497
